TPU v7x, 16 devices: a whole 2x2x2 slice. The times are simulated.
16 devices in a mesh: dp: 2 (over z), tp: 8 (over y, x, core).
Axes of the slice: x: 2, y: 2, z: 2, core: 2. Of those that a mesh axis runs over, the one named last changes fastest.
Arguments:
- y_one: float32 [16, 256, 1280], P('dp'), parts along dimension 0
- y_two: float32 [16, 256, 1280], P('dp'), parts along dimension 0
- dy_one: float32 [16, 256, 1280], P('dp'), parts along dimension 0
- dy_two: float32 [16, 256, 1280], P('dp'), parts along dimension 0
- saved_one: float32 [1, 16, 256, 1280], P(None, 'dp'), parts along dimension 1
- saved_two: float32 [1, 16, 256, 1280], P(None, 'dp'), parts along dimension 1
- w_qkv: bfloat16 [3, 1280, 3, 16, 80], P(None, None, None, 'tp')
- w_o: bfloat16 [3, 16, 80, 1280], P(None, 'tp')
- w_in: bfloat16 [3, 1280, 5120], P(None, None, 'tp')
- w_out: bfloat16 [3, 5120, 1280], P(None, 'tp')
Outputs:
- output 1: float32 [16, 256, 1280], P('dp'), parts along dimension 0
- output 2: float32 [16, 256, 1280], P('dp'), parts along dimension 0
- output 3: float32 [16, 256, 1280], P('dp'), parts along dimension 0
- output 4: float32 [16, 256, 1280], P('dp'), parts along dimension 0
- output 5: float32 [6, 1280, 3, 16, 80], P('dp', None, None, 'tp'), parts along dimension 0
- output 6: float32 [6, 16, 80, 1280], P('dp', 'tp'), parts along dimension 0
- output 7: float32 [6, 1280, 5120], P('dp', None, 'tp'), parts along dimension 0
- output 8: float32 [6, 5120, 1280], P('dp', 'tp'), parts along dimension 0
There are 2 independent parts. A program takes and returns all parts, laid end to end along the dimension named above; an argument that names none is the same for every part.
All inputs are finite; a program needn't handle non-finite values.
Results may differ from a plain program's by a relative error of at most 0.0121767.
Values are sent between devices in bfloat16 or wider.
A program may use at most 1 GiB of HBM per device.

v0:
```python
import jax
import jax.numpy as jnp
from jax import lax
from jax.sharding import PartitionSpec as P

EPS = 1e-6


def rms_norm(state):
    return state * lax.rsqrt(jnp.mean(state * state, axis=-1, keepdims=True) + EPS)


def gelu_tanh(hidden):
    return jax.nn.gelu(hidden, approximate=True)


def attn_forward(normed, w_qkv):
    head_dim = w_qkv.shape[-1]
    qkv_all = jnp.einsum("bsh,hkne->kbsne", normed, w_qkv, preferred_element_type=jnp.float32).astype(jnp.bfloat16)
    scores = jnp.einsum("bqne,bkne->bnqk", qkv_all[0], qkv_all[1], preferred_element_type=jnp.float32) * head_dim ** -0.5
    attn_probs = jax.nn.softmax(scores, axis=-1)
    probs_bf = attn_probs.astype(jnp.bfloat16)
    heads_out = jnp.einsum("bnqk,bkne->bqne", probs_bf, qkv_all[2], preferred_element_type=jnp.float32).astype(jnp.bfloat16)
    return qkv_all, attn_probs, probs_bf, heads_out


def attn_backward(normed, w_qkv, w_o, attn_cache, d_out):
    qkv_all, attn_probs, probs_bf, heads_out = attn_cache
    head_dim = w_qkv.shape[-1]
    d_bf = d_out.astype(jnp.bfloat16)
    d_wo = jnp.einsum("bqne,bqh->neh", heads_out, d_bf, preferred_element_type=jnp.float32)
    d_heads = jnp.einsum("bqh,neh->bqne", d_bf, w_o, preferred_element_type=jnp.float32).astype(jnp.bfloat16)
    d_v = jnp.einsum("bnqk,bqne->bkne", probs_bf, d_heads, preferred_element_type=jnp.float32)
    d_probs = jnp.einsum("bqne,bkne->bnqk", d_heads, qkv_all[2], preferred_element_type=jnp.float32)
    d_scores = attn_probs * (d_probs - jnp.sum(d_probs * attn_probs, axis=-1, keepdims=True)) * head_dim ** -0.5
    ds_bf = d_scores.astype(jnp.bfloat16)
    d_q = jnp.einsum("bnqk,bkne->bqne", ds_bf, qkv_all[1], preferred_element_type=jnp.float32)
    d_k = jnp.einsum("bnqk,bqne->bkne", ds_bf, qkv_all[0], preferred_element_type=jnp.float32)
    d_qkv = jnp.stack([d_q.astype(jnp.bfloat16), d_k.astype(jnp.bfloat16), d_v.astype(jnp.bfloat16)], axis=2)
    d_wqkv = jnp.einsum("bsh,bskne->hkne", normed, d_qkv, preferred_element_type=jnp.float32)
    d_normed = jnp.einsum("bskne,hkne->bsh", d_qkv, w_qkv, preferred_element_type=jnp.float32)
    return d_normed, d_wqkv, d_wo


def mlp_forward(normed, w_in):
    hidden = jnp.einsum("bsh,hf->bsf", normed, w_in, preferred_element_type=jnp.float32)
    gelu_out, gelu_pull = jax.vjp(gelu_tanh, hidden)
    return gelu_out.astype(jnp.bfloat16), gelu_pull


def mlp_backward(normed, w_in, w_out, act_bf, gelu_pull, d_out):
    d_bf = d_out.astype(jnp.bfloat16)
    d_wout = jnp.einsum("bsf,bsh->fh", act_bf, d_bf, preferred_element_type=jnp.float32)
    d_act = jnp.einsum("bsh,fh->bsf", d_bf, w_out, preferred_element_type=jnp.float32)
    d_hidden = gelu_pull(d_act)[0].astype(jnp.bfloat16)
    d_win = jnp.einsum("bsh,bsf->hf", normed, d_hidden, preferred_element_type=jnp.float32)
    d_normed = jnp.einsum("bsf,hf->bsh", d_hidden, w_in, preferred_element_type=jnp.float32)
    return d_normed, d_win, d_wout


def reversible_block(block_w, y_one, y_two, d_one, d_two, want_x_one):
    w_qkv, w_o, w_in, w_out = block_w
    g_norm, g_norm_pull = jax.vjp(rms_norm, y_one)
    g_in = g_norm.astype(jnp.bfloat16)
    act_bf, gelu_pull = mlp_forward(g_in, w_in)
    g_part = jnp.einsum("bsf,fh->bsh", act_bf, w_out, preferred_element_type=jnp.float32)
    x_two = y_two - lax.psum(g_part, "tp")
    g_back, d_win, d_wout = mlp_backward(g_in, w_in, w_out, act_bf, gelu_pull, d_two)
    d_one = d_one + g_norm_pull(lax.psum(g_back, "tp"))[0]
    f_norm, f_norm_pull = jax.vjp(rms_norm, x_two)
    f_in = f_norm.astype(jnp.bfloat16)
    attn_cache = attn_forward(f_in, w_qkv)
    x_one = None
    if want_x_one:
        f_part = jnp.einsum("bqne,neh->bqh", attn_cache[3], w_o, preferred_element_type=jnp.float32)
        x_one = y_one - lax.psum(f_part, "tp")
    f_back, d_wqkv, d_wo = attn_backward(f_in, w_qkv, w_o, attn_cache, d_one)
    d_two = d_two + f_norm_pull(lax.psum(f_back, "tp"))[0]
    return x_one, x_two, d_one, d_two, (d_wqkv, d_wo, d_win, d_wout)


def plain_block(block_w, x_one, x_two, d_one, d_two):
    w_qkv, w_o, w_in, w_out = block_w
    f_norm, f_norm_pull = jax.vjp(rms_norm, x_two)
    f_in = f_norm.astype(jnp.bfloat16)
    attn_cache = attn_forward(f_in, w_qkv)
    f_back, d_wqkv, d_wo = attn_backward(f_in, w_qkv, w_o, attn_cache, d_one)
    g_norm, g_norm_pull = jax.vjp(rms_norm, x_one)
    g_in = g_norm.astype(jnp.bfloat16)
    act_bf, gelu_pull = mlp_forward(g_in, w_in)
    g_back, d_win, d_wout = mlp_backward(g_in, w_in, w_out, act_bf, gelu_pull, d_two)
    new_one = d_one + g_norm_pull(lax.psum(g_back, "tp"))[0]
    new_two = d_two + f_norm_pull(lax.psum(f_back, "tp"))[0]
    return new_one, new_two, (d_wqkv, d_wo, d_win, d_wout)


def solution(mesh):
    act_spec = P("dp", None, None)
    saved_spec = P(None, "dp", None, None)
    weight_specs = (P(None, None, None, "tp", None), P(None, "tp", None, None), P(None, None, "tp"), P(None, "tp", None))
    grad_specs = (P("dp", None, None, "tp", None), P("dp", "tp", None, None), P("dp", None, "tp"), P("dp", "tp", None))

    def per_device(y_one, y_two, dy_one, dy_two, saved_one, saved_two, w_qkv, w_o, w_in, w_out):
        all_w = (w_qkv, w_o, w_in, w_out)
        n_layers = w_qkv.shape[0]
        n_pairs = saved_one.shape[0]
        grad_list = [None] * n_layers
        top_w = tuple(weight[n_layers - 1] for weight in all_w)
        x_one, x_two, d_one, d_two, top_grads = reversible_block(top_w, y_one, y_two, dy_one, dy_two, n_pairs == 0)
        grad_list[n_layers - 1] = top_grads
        for pair_idx in reversed(range(n_pairs)):
            plain_w = tuple(weight[2 * pair_idx + 1] for weight in all_w)
            d_one, d_two, plain_grads = plain_block(plain_w, saved_one[pair_idx], saved_two[pair_idx], d_one, d_two)
            grad_list[2 * pair_idx + 1] = plain_grads
            rev_w = tuple(weight[2 * pair_idx] for weight in all_w)
            x_one, x_two, d_one, d_two, rev_grads = reversible_block(rev_w, saved_one[pair_idx], saved_two[pair_idx], d_one, d_two, pair_idx == 0)
            grad_list[2 * pair_idx] = rev_grads
        stacked = tuple(jnp.stack([entry[slot_idx] for entry in grad_list]) for slot_idx in range(4))
        return (x_one, x_two, d_one, d_two) + stacked

    return jax.shard_map(
        per_device,
        mesh=mesh,
        in_specs=(act_spec,) * 4 + (saved_spec,) * 2 + weight_specs,
        out_specs=(act_spec,) * 4 + grad_specs,
        check_vma=False,
    )
```

profile of v0, /device:TPU:0, one launch (start us, length us, event | category | flops | bytes accessed | tf_op | source)
XLA Modules:
  0.0 1493.6 jit_solution(4669314088222955906)
XLA Ops:
  7.2 4.9 multiply_reduce_fusion.4
  14.2 6.2 fusion.152
  22.8 7.7 fusion.168
  30.5 8.4 fusion.32
  40.4 8.3 fusion.165
  49.0 4.7 fusion.12
  53.7 7.1 convert_bitcast_fusion
  61.6 3.2 fusion.323
  67.3 239.3 %all-reduce.15.cloned.1.call-done = (f32[8,256,1280]{2,1,0:T(8,128)}, f32[8,256,1280]{2,1,0:T(8,128)}) async-done(((f32[8,256,1280]{2,1,0:T(8,128)}, f32[8,256,1280]{2,1,0:T(8,128)}), (f32[8,256,1280]{2,1,0:T(8,128)}, f32[8,256,1280]{2,1,0:T(8,128)})) %all-reduce.15.cloned.1.call-update) | async-done | bytes 20971536 | tf_op jit(solution)/shard_map/psum | solution.py:69
  306.7 7.9 multiply_reduce_fusion.3
  314.6 25.2 %multiply_reduce_fusion.2 = (f32[8,256]{1,0:T(8,128)S(1)}, f32[8,256,1280]{2,1,0:T(8,128)}, bf16[8,256,1280]{2,1,0:T(8,128)(2,1)S(1)}, f32[8,256,1280]{2,1,0:T(8,128)}) fusion(f32[8,256,1280]{2,1,0:T(8,128)} %param.11, f32[8,256,1280]{2,1,0:T(8,128)} %get-tuple-element.18, f32[8,256,1280]{2,1,0:T(8,128)} %param.12, f32[8,256,1280]{2,1,0:T(8,128)} %param.10, ...), kind=kLoop, calls=%fused_computation.41 | loop fusion | flops 23590912 | bytes 78667776 | tf_op jit(solution)/shard_map/jvp()/reduce_sum | solution.py:10
  343.6 3.9 fusion.316
  347.5 8.3 fusion.230
  355.7 8.3 fusion.227
  364.0 7.1 convert_bitcast_fusion.1
  371.9 2.8 fusion.315
  374.7 3.1 fusion.322
  377.8 8.3 fusion.221
  386.1 8.7 fusion.224
  400.8 5.6 convolution_bitcast_fusion.2
  406.5 5.5 convolution_bitcast_fusion.1
  412.0 4.7 fusion.15
  416.8 7.7 fusion.150
  424.5 10.5 fusion.172
  435.1 7.5 fusion.148
  442.6 224.4 %all-reduce.13.cloned.1.call-done = (f32[8,256,1280]{2,1,0:T(8,128)}, f32[8,256,1280]{2,1,0:T(8,128)}) async-done(((f32[8,256,1280]{2,1,0:T(8,128)}, f32[8,256,1280]{2,1,0:T(8,128)}), (f32[8,256,1280]{2,1,0:T(8,128)}, f32[8,256,1280]{2,1,0:T(8,128)})) %all-reduce.13.cloned.1.call-update) | async-done | bytes 20971536 | tf_op jit(solution)/shard_map/psum | solution.py:78
  667.0 7.9 multiply_reduce_fusion.1
  675.0 7.9 fusion.13
  683.0 17.3 %fusion.10 = (f32[8,256,1280]{2,1,0:T(8,128)S(1)}, bf16[8,256,1280]{2,1,0:T(8,128)(2,1)S(1)}) fusion(f32[1,8,256,1280]{3,2,1,0:T(8,128)} %param.15, f32[8,256,1280]{2,1,0:T(8,128)} %get-tuple-element.16, f32[8,256]{1,0:T(8,128)S(1)} %multiply_multiply_fusion.8, f32[8,256]{1,0:T(8,128)S(1)} %fusion.289, f32[8,256,1280]{2,1,0:T(8,128)} %param.13, ...), kind=kLoop, calls=%fused_computation.16 | loop fusion | flops 28835840 | bytes 68190208 | tf_op jit(solution)/shard_map/add | solution.py:93
  700.3 12.1 fusion.25
  712.5 9.8 fusion.39
  722.3 9.2 fusion.161
  731.5 8.3 fusion.174
  740.5 10.9 convolution_bitcast_fusion.7
  751.4 11.2 convolution_bitcast_fusion.4
  762.6 5.0 fusion.114
  767.6 339.2 %all-reduce.11.cloned.1.call-done = (f32[8,256,1280]{2,1,0:T(8,128)}, f32[8,256,1280]{2,1,0:T(8,128)}, f32[8,256,1280]{2,1,0:T(8,128)}) async-done(((f32[8,256,1280]{2,1,0:T(8,128)}, f32[8,256,1280]{2,1,0:T(8,128)}, f32[8,256,1280]{2,1,0:T(8,128)}), (f32[8,256,1280]{2,1,0:T(8,128)}, f32[8,256,1280]{2,1,0:T(8,128)}, f32[8,256,1280]{2,1,0:T(8,128)})) %all-reduce.11.cloned.1.call-update) | async-done | bytes 31457296 | tf_op jit(solution)/shard_map/psum | solution.py:67
  1106.9 12.8 multiply_reduce_fusion.5
  1123.8 6.0 fusion.16
  1129.8 11.6 fusion.9
  1141.5 3.3 fusion.218
  1149.3 4.2 convert_bitcast_fusion.2
  1154.2 2.8 fusion.265
  1157.0 3.1 fusion.324
  1163.0 8.3 fusion.236
  1171.3 8.2 fusion.233
  1179.5 2.7 fusion.239
  1182.2 6.8 convolution_bitcast_fusion.3
  1189.0 6.9 convolution_bitcast_fusion
  1195.9 5.8 fusion.111
  1201.8 8.8 fusion.81
  1210.6 4.5 fusion.87
  1215.1 6.6 convolution_bitcast_fusion.9
  1221.8 5.0 convolution_bitcast_fusion.8
  1226.8 4.5 pad_maximum_fusion
  1231.3 8.3 convolution_bitcast_fusion.5
  1239.6 11.6 convolution_bitcast_fusion.6
  1251.2 7.6 pad_maximum_fusion.1
  1262.6 7.1 fusion.84
  1269.7 3.7 pad_maximum_fusion.2
  1273.4 177.8 %all-reduce.9.cloned.1.call-done = (f32[8,256,1280]{2,1,0:T(8,128)}, f32[8,256,1280]{2,1,0:T(8,128)}) async-done(((f32[8,256,1280]{2,1,0:T(8,128)}, f32[8,256,1280]{2,1,0:T(8,128)}), (f32[8,256,1280]{2,1,0:T(8,128)}, f32[8,256,1280]{2,1,0:T(8,128)})) %all-reduce.9.cloned.1.call-update) | async-done | bytes 20971536 | tf_op jit(solution)/shard_map/psum | solution.py:76
  1451.1 12.4 bitcast_subtract_fusion.1
  1463.5 8.0 multiply_reduce_fusion
  1471.5 15.1 %fusion.11 = f32[8,256,1280]{2,1,0:T(8,128)} fusion(f32[8,256,1280]{2,1,0:T(8,128)} %copy-done.3, f32[8,256,1280]{2,1,0:T(8,128)} %get-tuple-element.20, f32[8,256,1280]{2,1,0:T(8,128)} %get-tuple-element.11, f32[8,256]{1,0:T(8,128)S(1)} %multiply_multiply_fusion.6, f32[8,256]{1,0:T(8,128)S(1)} %copy-done.27), kind=kLoop, calls=%fused_computation.17 | loop fusion | flops 13107200 | bytes 41959424 | tf_op jit(solution)/shard_map/add | solution.py:78
  (191 shorter events, 36.7 us)
Async XLA Ops:
  7.2 299.5 %all-reduce.15.cloned.1.call-start = ((), (), s32[]{:S(2)}) async-start(), calls=%async_computation.3 | async-start | bytes 41943040 | tf_op jit(solution)/shard_map/psum | solution.py:69
  7.2 7.0 copy-start.2
  7.2 15.6 %slice-start.23 = ((s8[4915200]{0:T(1024)(128)(4,1)}), s8[4194304]{0:T(1024)(128)(4,1)S(1)}, s32[]{:S(2)}) async-start(s8[4915200]{0:T(1024)(128)(4,1)} %bitcast.384), calls=%async_computation.27 | async-start | bytes 8388608
  14.2 300.4 %copy-start.24 = (f32[8,256]{1,0:T(8,128)}, f32[8,256]{1,0:T(8,128)S(1)}, u32[]{:S(2)}) copy-start(f32[8,256]{1,0:T(8,128)S(1)} %fusion.287) | copy-start | bytes 24580
  14.2 8.6 slice-start.24
  14.2 16.3 %slice-start.18 = ((s8[10485760]{0:T(1024)(128)(4,1)}), s8[2097152]{0:T(1024)(128)(4,1)S(1)}, s32[]{:S(2)}) async-start(s8[10485760]{0:T(1024)(128)(4,1)} %bitcast.380), calls=%async_computation.22 | async-start | bytes 4194304
  14.2 16.3 %slice-start.19 = ((s8[10485760]{0:T(1024)(128)(4,1)}), s8[4194304]{0:T(1024)(128)(4,1)S(1)}, s32[]{:S(2)}) async-start(s8[10485760]{0:T(1024)(128)(4,1)} %bitcast.380), calls=%async_computation.23 | async-start | bytes 8388608
  22.8 7.7 slice-start.20
  48.8 618.3 %all-reduce.13.cloned.1.call-start = ((), (), s32[]{:S(2)}) async-start(), calls=%async_computation.2 | async-start | bytes 41943040 | tf_op jit(solution)/shard_map/psum | solution.py:78
  53.7 629.2 %copy-start.28 = (f32[8,256]{1,0:T(8,128)}, f32[8,256]{1,0:T(8,128)S(1)}, u32[]{:S(2)}) copy-start(f32[8,256]{1,0:T(8,128)S(1)} %fusion.289) | copy-start | bytes 24580
  60.8 4.0 copy-start.14
  314.6 25.3 %copy-start.21 = (bf16[3,2,80,1280]{3,2,1,0:T(8,128)(2,1)S(1)}, bf16[3,2,80,1280]{3,2,1,0:T(8,128)(2,1)}, u32[]{:S(2)}) copy-start(bf16[3,2,80,1280]{3,2,1,0:T(8,128)(2,1)} %param.17) | copy-start | bytes 3686404
  364.0 318.9 %copy-start.30 = (f32[8,256]{1,0:T(8,128)}, f32[8,256]{1,0:T(8,128)S(1)}, u32[]{:S(2)}) copy-start(f32[8,256]{1,0:T(8,128)S(1)} %fusion.288) | copy-start | bytes 24580
  397.4 9.1 copy-start.5
  398.2 8.3 copy-start.19
  400.8 5.7 copy-start.17
  400.8 5.7 copy-start.41
  400.8 5.7 copy-start.42
  412.0 694.9 %all-reduce.11.cloned.1.call-start = ((), (), s32[]{:S(2)}) async-start(), calls=%async_computation.1 | async-start | bytes 62914560 | tf_op jit(solution)/shard_map/psum | solution.py:67
  416.8 18.3 %slice-start = ((s8[10485760]{0:T(1024)(128)(4,1)}), s8[4194304]{0:T(1024)(128)(4,1)S(1)}, s32[]{:S(2)}) async-start(s8[10485760]{0:T(1024)(128)(4,1)} %bitcast.368), calls=%async_computation.4 | async-start | bytes 8388608
  416.8 18.3 %slice-start.1 = ((s8[10485760]{0:T(1024)(128)(4,1)}), s8[4194304]{0:T(1024)(128)(4,1)S(1)}, s32[]{:S(2)}) async-start(s8[10485760]{0:T(1024)(128)(4,1)} %bitcast.368), calls=%async_computation.5 | async-start | bytes 8388608
  424.5 10.5 copy-start.33
  424.5 10.5 slice-start.2
  700.3 12.2 copy-start.3
  700.3 12.2 copy-start.7
  712.5 19.0 %copy-start.38 = (bf16[8,256,640]{2,1,0:T(8,128)(2,1)}, bf16[8,256,640]{2,1,0:T(8,128)(2,1)S(1)}, u32[]{:S(2)}) copy-start(bf16[8,256,640]{2,1,0:T(8,128)(2,1)S(1)} %fusion.25) | copy-start | bytes 7864324
  722.3 9.2 copy-start.36
  739.8 711.3 %all-reduce.9.cloned.1.call-start = ((), (), s32[]{:S(2)}) async-start(), calls=%async_computation | async-start | bytes 41943040 | tf_op jit(solution)/shard_map/psum | solution.py:76
  1106.9 12.8 slice-start.3
  1106.9 12.8 slice-start.15
  1106.9 14.5 slice-start.4
  1106.9 15.1 %slice-start.5 = ((s8[10485760]{0:T(1024)(128)(4,1)}), s8[2097152]{0:T(1024)(128)(4,1)S(1)}, s32[]{:S(2)}) async-start(s8[10485760]{0:T(1024)(128)(4,1)} %bitcast.370), calls=%async_computation.9 | async-start | bytes 4194304
  1106.9 16.3 %slice-start.16 = ((s8[10485760]{0:T(1024)(128)(4,1)}), s8[4194304]{0:T(1024)(128)(4,1)S(1)}, s32[]{:S(2)}) async-start(s8[10485760]{0:T(1024)(128)(4,1)} %bitcast.378), calls=%async_computation.20 | async-start | bytes 8388608
  1106.9 16.9 %slice-start.17 = ((s8[10485760]{0:T(1024)(128)(4,1)}), s8[2097152]{0:T(1024)(128)(4,1)S(1)}, s32[]{:S(2)}) async-start(s8[10485760]{0:T(1024)(128)(4,1)} %bitcast.378), calls=%async_computation.21 | async-start | bytes 4194304
  1119.7 10.1 copy-start.22
  1119.7 27.1 %copy-start.26 = (f32[8,256]{1,0:T(8,128)}, f32[8,256]{1,0:T(8,128)S(1)}, u32[]{:S(2)}) copy-start(f32[8,256]{1,0:T(8,128)S(1)} %fusion.286) | copy-start | bytes 24580
  1141.4 5.3 copy-start
  1141.4 7.9 copy-start.1
  1163.0 26.0 %copy-start.39 = (bf16[8,256,1,2,80]{1,4,3,0,2:T(8,128)(2,1)}, bf16[8,256,1,2,80]{1,4,3,0,2:T(8,128)(2,1)S(1)}, u32[]{:S(2)}) copy-start(bf16[8,256,1,2,80]{1,4,3,0,2:T(8,128)(2,1)S(1)} %fusion.242) | copy-start | bytes 1966084
  1182.2 6.8 copy-start.47
  1182.2 6.8 copy-start.49
  1195.9 5.8 copy-start.20
  1195.9 5.8 copy-start.29
  1195.9 14.6 slice-start.12
  1201.7 8.8 slice-start.13
  1201.7 8.8 slice-start.14
  1201.7 8.8 copy-start.18
  1201.7 8.8 copy-start.31
  1201.7 8.8 copy-start.44
  1201.8 8.8 copy-start.46
  1201.8 13.3 slice-start.6
  1201.8 13.3 slice-start.7
  1210.6 4.5 slice-start.8
  1215.1 6.7 copy-start.37
  1215.1 16.2 %slice-start.21 = ((s8[5242880]{0:T(1024)(128)(4,1)}), s8[4194304]{0:T(1024)(128)(4,1)S(1)}, s32[]{:S(2)}) async-start(s8[5242880]{0:T(1024)(128)(4,1)} %bitcast.382), calls=%async_computation.25 | async-start | bytes 8388608
  1221.8 5.0 copy-start.10
  1221.8 9.5 slice-start.22
  1239.6 11.6 copy-start.9
  1239.6 19.2 %slice-start.9 = ((s8[10485760]{0:T(1024)(128)(4,1)}), s8[4194304]{0:T(1024)(128)(4,1)S(1)}, s32[]{:S(2)}) async-start(s8[10485760]{0:T(1024)(128)(4,1)} %bitcast.374), calls=%async_computation.13 | async-start | bytes 8388608
  1239.6 19.2 %slice-start.10 = ((s8[10485760]{0:T(1024)(128)(4,1)}), s8[4194304]{0:T(1024)(128)(4,1)S(1)}, s32[]{:S(2)}) async-start(s8[10485760]{0:T(1024)(128)(4,1)} %bitcast.374), calls=%async_computation.14 | async-start | bytes 8388608
  1251.2 7.6 slice-start.11
  1262.6 7.1 copy-start.11
  1262.6 7.1 copy-start.12
  1463.5 8.0 copy-start.23
  (16 other events, 35.4 us)
Sparse Core Ops, SparseCore 0:
  48.9 257.7 all-reduce.14
  412.1 254.9 all-reduce.12
  740.0 366.8 all-reduce.10
  1196.0 255.0 all-reduce.8
where the time goes:
time: 1510 us; the launch traced here: 1490 us
  waiting for transfers between devices  981 us (65%)
  matrix products  298 us (20%)
  other arithmetic  177 us (12%)
  local copies, waits for them, and re-layouts  22.2 us (1%)
  between operations  15.1 us (1%)
    psum x1, waiting for transfers between devices, reversible_block(): x_two = y_two - lax.psum(g_part, 'tp')  339 us
    psum x1, waiting for transfers between devices, reversible_block(): d_one = d_one + g_norm_pull(lax.psum(g_back, 'tp'))[0]  239 us
    psum x1, waiting for transfers between devices, reversible_block(): d_two = d_two + f_norm_pull(lax.psum(f_back, 'tp'))[0]  224 us
    psum x1, waiting for transfers between devices, reversible_block(): x_one = y_one - lax.psum(f_part, 'tp')  178 us
    reduce_sum x5, other arithmetic, rms_norm(): jnp.mean(state * state, axis=-1, keepdims=True) + EPS  52.4 us
    reduce_sum x5, other arithmetic, rms_norm(): state * lax.rsqrt(jnp.mean(state * state, axis=-1, keepdims=True) + EPS)  37.8 us
    dot_general x3, matrix products, mlp_backward(): jnp.einsum('bsf,bsh->fh', act_bf, d_bf, preferred_element_type=jnp.float32)  31.1 us
    dot_general x3, matrix products, mlp_backward(): jnp.einsum('bsh,fh->bsf', d_bf, w_out, preferred_element_type=jnp.float32)  30.3 us
  transfers between devices with their start and end apart: 4, of which 4 were waited for; matrix products, arithmetic and copies ran while one was open for 10% of the time, Pallas kernels for 0%

commit v1 on v0

v1 whole, which is shorter than its diff:
```python
import jax
import jax.numpy as jnp
from jax import lax
from jax.sharding import PartitionSpec as P

EPS = 1e-6
BF = jnp.bfloat16
F32 = jnp.float32


def rms_norm(state):
    return state * lax.rsqrt(jnp.mean(state * state, axis=-1, keepdims=True) + EPS)


def rms_vjp(state, cot):
    rinv = lax.rsqrt(jnp.mean(state * state, axis=-1, keepdims=True) + EPS)
    normed = state * rinv
    return rinv * (cot - normed * jnp.mean(cot * normed, axis=-1, keepdims=True))


def gelu_tanh(hidden):
    return jax.nn.gelu(hidden, approximate=True)


def mm(spec, left, right):
    return jnp.einsum(spec, left, right, preferred_element_type=F32)


def attn_forward(normed, w_qkv):
    head_dim = w_qkv.shape[-1]
    qkv_all = mm("bsh,hkne->kbsne", normed, w_qkv).astype(BF)
    scores = mm("bqne,bkne->bnqk", qkv_all[0], qkv_all[1]) * head_dim ** -0.5
    attn_probs = jax.nn.softmax(scores, axis=-1)
    probs_bf = attn_probs.astype(BF)
    heads_out = mm("bnqk,bkne->bqne", probs_bf, qkv_all[2]).astype(BF)
    return qkv_all, attn_probs, probs_bf, heads_out


def attn_backward(normed, w_qkv, w_o, attn_cache, d_bf):
    qkv_all, attn_probs, probs_bf, heads_out = attn_cache
    head_dim = w_qkv.shape[-1]
    d_wo = mm("bqne,bqh->neh", heads_out, d_bf)
    d_heads = mm("bqh,neh->bqne", d_bf, w_o).astype(BF)
    d_v = mm("bnqk,bqne->bkne", probs_bf, d_heads)
    d_probs = mm("bqne,bkne->bnqk", d_heads, qkv_all[2])
    d_scores = attn_probs * (d_probs - jnp.sum(d_probs * attn_probs, axis=-1, keepdims=True)) * head_dim ** -0.5
    ds_bf = d_scores.astype(BF)
    d_q = mm("bnqk,bkne->bqne", ds_bf, qkv_all[1])
    d_k = mm("bnqk,bqne->bkne", ds_bf, qkv_all[0])
    d_qkv = jnp.stack([d_q.astype(BF), d_k.astype(BF), d_v.astype(BF)], axis=2)
    d_wqkv = mm("bsh,bskne->hkne", normed, d_qkv)
    d_normed = mm("bskne,hkne->bsh", d_qkv, w_qkv)
    return d_normed, d_wqkv, d_wo


def mlp_forward(normed, w_in):
    hidden = mm("bsh,hf->bsf", normed, w_in)
    gelu_out, gelu_pull = jax.vjp(gelu_tanh, hidden)
    return gelu_out.astype(BF), gelu_pull


def mlp_backward(normed, w_in, w_out, act_bf, gelu_pull, d_bf):
    d_wout = mm("bsf,bsh->fh", act_bf, d_bf)
    d_act = mm("bsh,fh->bsf", d_bf, w_out)
    d_hidden = gelu_pull(d_act)[0].astype(BF)
    d_win = mm("bsh,bsf->hf", normed, d_hidden)
    d_normed = mm("bsf,hf->bsh", d_hidden, w_in)
    return d_normed, d_win, d_wout


def scatter_sum(part):
    return lax.psum_scatter(part, "tp", scatter_dimension=0, tiled=True)


def gather(shard):
    return lax.all_gather(shard, "tp", axis=0, tiled=True)


def solution(mesh):
    act_spec = P("dp", None, None)
    saved_spec = P(None, "dp", None, None)
    weight_specs = (P(None, None, None, "tp", None), P(None, "tp", None, None), P(None, None, "tp"), P(None, "tp", None))
    grad_specs = (P("dp", None, None, "tp", None), P("dp", "tp", None, None), P("dp", None, "tp"), P("dp", "tp", None))
    n_tp = mesh.shape["tp"]

    def per_device(y_one, y_two, dy_one, dy_two, saved_one, saved_two, w_qkv, w_o, w_in, w_out):
        rank = lax.axis_index("tp")
        rows = y_one.shape[0] // n_tp

        def shard(full):
            return lax.dynamic_slice_in_dim(full, rank * rows, rows, axis=0)

        n_layers = w_qkv.shape[0]
        grads = [None] * n_layers
        top = n_layers - 1
        in_bf = rms_norm(y_one).astype(BF)
        act_bf, pull = mlp_forward(in_bf, w_in[top])
        g_sum = scatter_sum(mm("bsf,fh->bsh", act_bf, w_out[top]))
        x_two = shard(y_two) - g_sum
        f_in = gather(rms_norm(x_two).astype(BF))
        g_back, d_win, d_wout = mlp_backward(in_bf, w_in[top], w_out[top], act_bf, pull, dy_two.astype(BF))
        d_one = shard(dy_one) + rms_vjp(shard(y_one), scatter_sum(g_back.astype(BF)).astype(F32))
        d_one_bf = gather(d_one.astype(BF))
        cache = attn_forward(f_in, w_qkv[top])
        f_back, d_wqkv, d_wo = attn_backward(f_in, w_qkv[top], w_o[top], cache, d_one_bf)
        d_two = shard(dy_two) + rms_vjp(x_two, scatter_sum(f_back.astype(BF)).astype(F32))
        d_two_bf = gather(d_two.astype(BF))
        grads[top] = (d_wqkv, d_wo, d_win, d_wout)
        for pair_idx in reversed(range(saved_one.shape[0])):
            s_one, s_two = saved_one[pair_idx], saved_two[pair_idx]
            hi, lo = 2 * pair_idx + 1, 2 * pair_idx
            s1_bf = rms_norm(s_one).astype(BF)
            s2_bf = rms_norm(s_two).astype(BF)
            cache = attn_forward(s2_bf, w_qkv[hi])
            f_back, d_wqkv, d_wo = attn_backward(s2_bf, w_qkv[hi], w_o[hi], cache, d_one_bf)
            act_bf, pull = mlp_forward(s1_bf, w_in[hi])
            g_back_hi, d_win, d_wout = mlp_backward(s1_bf, w_in[hi], w_out[hi], act_bf, pull, d_two_bf)
            grads[hi] = (d_wqkv, d_wo, d_win, d_wout)
            d_two = d_two + rms_vjp(shard(s_two), scatter_sum(f_back.astype(BF)).astype(F32))
            d_two_bf = gather(d_two.astype(BF))
            act_bf, pull = mlp_forward(s1_bf, w_in[lo])
            g_sum = scatter_sum(mm("bsf,fh->bsh", act_bf, w_out[lo]))
            x_two = shard(s_two) - g_sum
            x_two_full = gather(x_two)
            f_in = rms_norm(x_two_full).astype(BF)
            g_back, d_win, d_wout = mlp_backward(s1_bf, w_in[lo], w_out[lo], act_bf, pull, d_two_bf)
            d_one = d_one + rms_vjp(shard(s_one), scatter_sum((g_back + g_back_hi).astype(BF)).astype(F32))
            d_one_bf = gather(d_one.astype(BF))
            cache = attn_forward(f_in, w_qkv[lo])
            if pair_idx == 0:
                heads_all = lax.all_gather(cache[3], "tp", axis=0, tiled=False)
                wo_all = lax.all_gather(w_o[lo], "tp", axis=0, tiled=False)
                x_one_full = s_one - mm("dbqne,dneh->bqh", heads_all, wo_all)
            f_back, d_wqkv, d_wo = attn_backward(f_in, w_qkv[lo], w_o[lo], cache, d_one_bf)
            d_two = d_two + rms_vjp(x_two, scatter_sum(f_back.astype(BF)).astype(F32))
            grads[lo] = (d_wqkv, d_wo, d_win, d_wout)
            if pair_idx:
                d_two_bf = gather(d_two.astype(BF))
        stacked = tuple(jnp.stack([entry[slot] for entry in grads]) for slot in range(4))
        return (x_one_full, x_two_full, gather(d_one), gather(d_two)) + stacked

    return jax.shard_map(
        per_device,
        mesh=mesh,
        in_specs=(act_spec,) * 4 + (saved_spec,) * 2 + weight_specs,
        out_specs=(act_spec,) * 4 + grad_specs,
        check_vma=False,
    )
```

time: 1510 us -> 1000 us (0.66)
  waiting for transfers between devices: 981 us -> 535 us
  other arithmetic: 177 us -> 82.5 us
  local copies, waits for them, and re-layouts: 22.2 us -> 43.7 us
  matrix products: 298 us -> 316 us
    psum x4 -> x0, waiting for transfers between devices: 981 us -> none  [the longest x1 339 us: reversible_block(): x_two = y_two - lax.psum(g_part, 'tp')]
    reduce_scatter x0 -> x7, waiting for transfers between devices: none -> 324 us  [scatter_sum(): return lax.psum_scatter(part, 'tp', scatter_dimension=0, tiled=True)]
    all_gather x0 -> x10, waiting for transfers between devices: none -> 209 us  [the longest x8 209 us: gather(): return lax.all_gather(shard, 'tp', axis=0, tiled=True)]
    add x3 -> x1, other arithmetic: 44.1 us -> 2.48 us  [per_device(): d_two = d_two + rms_vjp(x_two, scatter_sum(f_back.astype(BF)).astype(F32))]
    reduce_sum x5 -> x4, other arithmetic: 52.4 us -> 19.2 us  [rms_norm(): jnp.mean(state * state, axis=-1, keepdims=True) + EPS]
    reduce_sum x5 -> x9, other arithmetic: 37.8 us -> 14.7 us  [the longest x5 8.35 us: rms_vjp(): jnp.mean(cot * normed, axis=-1, keepdims=True)]
    unnamed x152 -> x119, local copies, waits for them, and re-layouts: 22.2 us -> 41.9 us
    dot_general x49, matrix products: 298 us -> 316 us  [mm(): return jnp.einsum(spec, left, right, preferred_element_type=F32)]
  transfers between devices with their start and end apart: 4 -> 17, of which waited for: 4 -> 13; matrix products, arithmetic and copies ran while one was open for 10% -> 32% of each run, Pallas kernels for 0% -> 0%
where the time goes in v1:
time: 1000 us; the launch traced here: 994 us
  waiting for transfers between devices  535 us (54%)
  matrix products  316 us (32%)
  other arithmetic  82.5 us (8%)
  local copies, waits for them, and re-layouts  43.7 us (4%)
  between operations  15.2 us (2%)
    reduce_scatter x7, waiting for transfers between devices, scatter_sum(): return lax.psum_scatter(part, 'tp', scatter_dimension=0, tiled=True)  324 us
    dot_general x49, matrix products, mm(): return jnp.einsum(spec, left, right, preferred_element_type=F32)  316 us
    all_gather x8, waiting for transfers between devices, gather(): return lax.all_gather(shard, 'tp', axis=0, tiled=True)  209 us
    unnamed x119, local copies, waits for them, and re-layouts  41.9 us
    another operation x4, other arithmetic, per_device(): jnp.stack([entry[slot] for entry in grads])  20.4 us
  transfers between devices with their start and end apart: 17, of which 13 were waited for; matrix products, arithmetic and copies ran while one was open for 32% of the time, Pallas kernels for 0%

profile of v1, /device:TPU:0, one launch (start us, length us, event | category | flops | bytes accessed | tf_op | source)
XLA Modules:
  0.0 994.5 jit_solution(14418094464183522164)
XLA Ops:
  7.2 4.9 multiply_reduce_fusion
  14.2 7.7 fusion.138
  21.9 8.9 fusion.23
  32.3 7.4 convolution_convert_fusion
  39.8 12.2 %fusion.152 = f32[8,256,1280]{2,1,0:T(8,128)} fusion(bf16[3,640,1280]{2,1,0:T(8,128)(2,1)} %param.19, f32[8,256,640]{2,1,0:T(8,128)} %fusion.138), kind=kOutput, calls=%fused_computation.160 | convolution fusion | flops 3367239680 | bytes 17367040 | tf_op jit(solution)/shard_map/bsf,fh->bsh/dot_general | solution.py:26
  53.8 39.3 %reduce-scatter.10.cloned.1.call-done = bf16[1,256,1280]{2,1,0:T(8,128)(2,1)} async-done(((bf16[8,256,1280]{2,1,0:T(8,128)(2,1)}), bf16[1,256,1280]{2,1,0:T(8,128)(2,1)}) %reduce-scatter.10.cloned.1.call-update) | async-done | bytes 655376 | tf_op jit(solution)/shard_map/reduce_scatter | solution.py:72
  98.2 74.2 %reduce-scatter.12.cloned.1.call-done = f32[1,256,1280]{2,1,0:T(8,128)} async-done(((f32[8,256,1280]{2,1,0:T(8,128)}), f32[1,256,1280]{2,1,0:T(8,128)}) %reduce-scatter.12.cloned.1.call-update) | async-done | bytes 1310736 | tf_op jit(solution)/shard_map/reduce_scatter | solution.py:72
  175.4 4.7 fusion.6
  180.1 7.1 convert_bitcast_fusion
  193.7 18.0 %all-gather.18.cloned.1.call-done = bf16[8,256,1280]{2,1,0:T(8,128)(2,1)} async-done(((bf16[1,256,1280]{2,1,0:T(8,128)(2,1)}), bf16[8,256,1280]{2,1,0:T(8,128)(2,1)}) %all-gather.18.cloned.1.call-update) | async-done | bytes 5242896 | tf_op jit(solution)/shard_map/all_gather | solution.py:76
  211.8 4.4 fusion.199
  217.0 3.9 fusion.310
  220.9 8.3 fusion.231
  229.1 8.3 fusion.228
  240.2 7.0 bitcast_convert_fusion.1
  247.5 4.4 fusion.196
  251.9 5.6 convert_bitcast_fusion.1
  264.1 7.4 fusion.225
  271.5 7.6 fusion.222
  285.0 5.9 bitcast_convert_fusion.2
  291.4 4.7 fusion.8
  296.2 7.6 fusion.136
  306.1 9.1 fusion.156
  318.8 40.7 %reduce-scatter.14.cloned.1.call-done = bf16[1,256,1280]{2,1,0:T(8,128)(2,1)} async-done(((bf16[8,256,1280]{2,1,0:T(8,128)(2,1)}), bf16[1,256,1280]{2,1,0:T(8,128)(2,1)}) %reduce-scatter.14.cloned.1.call-update) | async-done | bytes 655376 | tf_op jit(solution)/shard_map/reduce_scatter | solution.py:72
  360.8 77.8 %reduce-scatter.8.cloned.1.call-done = f32[1,256,1280]{2,1,0:T(8,128)} async-done(((f32[8,256,1280]{2,1,0:T(8,128)}), f32[1,256,1280]{2,1,0:T(8,128)}) %reduce-scatter.8.cloned.1.call-update) | async-done | bytes 1310736 | tf_op jit(solution)/shard_map/reduce_scatter | solution.py:72
  438.7 4.6 fusion.317
  444.1 11.1 %fusion.134 = f32[8,256,640]{2,1,0:T(8,128)} fusion(f32[1,8,256,1280]{3,2,1,0:T(8,128)} %param.14, f32[8,256]{1,0:T(8,128)S(1)} %add_rsqrt_fusion.3, bf16[3,1280,640]{2,1,0:T(8,128)(2,1)} %param.18), kind=kOutput, calls=%fused_computation.146 | convolution fusion | flops 3360686080 | bytes 17375232 | tf_op jit(solution)/shard_map/bsh,hf->bsf/dot_general | solution.py:26
  455.1 25.2 %all-gather.20.cloned.1.call-done = bf16[8,256,1280]{2,1,0:T(8,128)(2,1)} async-done(((bf16[1,256,1280]{2,1,0:T(8,128)(2,1)}), bf16[8,256,1280]{2,1,0:T(8,128)(2,1)}) %all-gather.20.cloned.1.call-update) | async-done | bytes 5242896 | tf_op jit(solution)/shard_map/all_gather | solution.py:76
  480.4 9.7 fusion.16
  491.6 8.3 fusion.158
  499.9 19.9 %all-gather.22.cloned.1.call-done = bf16[8,256,1280]{2,1,0:T(8,128)(2,1)} async-done(((bf16[1,256,1280]{2,1,0:T(8,128)(2,1)}), bf16[8,256,1280]{2,1,0:T(8,128)(2,1)}) %all-gather.22.cloned.1.call-update) | async-done | bytes 5242896 | tf_op jit(solution)/shard_map/all_gather | solution.py:76
  519.8 9.7 fusion.30
  531.0 7.5 add_convert_fusion
  540.7 48.3 %reduce-scatter.18.cloned.1.call-done = bf16[1,256,1280]{2,1,0:T(8,128)(2,1)} async-done(((bf16[8,256,1280]{2,1,0:T(8,128)(2,1)}), bf16[1,256,1280]{2,1,0:T(8,128)(2,1)}) %reduce-scatter.18.cloned.1.call-update) | async-done | bytes 655376 | tf_op jit(solution)/shard_map/reduce_scatter | solution.py:72
  590.9 4.2 fusion.315
  595.4 54.8 %all-gather.12.cloned.1.call-done = f32[8,256,1280]{2,1,0:T(8,128)} async-done(((f32[1,256,1280]{2,1,0:T(8,128)}), f32[8,256,1280]{2,1,0:T(8,128)}) %all-gather.12.cloned.1.call-update) | async-done | bytes 10485776 | tf_op jit(solution)/shard_map/all_gather | solution.py:76
  650.1 4.9 multiply_reduce_fusion.1
  657.1 4.1 convert_bitcast_fusion.2
  666.4 23.0 %all-gather.26.cloned.1.call-done = bf16[8,256,1280]{2,1,0:T(8,128)(2,1)} async-done(((bf16[1,256,1280]{2,1,0:T(8,128)(2,1)}), bf16[8,256,1280]{2,1,0:T(8,128)(2,1)}) %all-gather.26.cloned.1.call-update) | async-done | bytes 5242896 | tf_op jit(solution)/shard_map/all_gather | solution.py:76
  689.4 4.4 fusion.202
  693.8 3.9 fusion.266
  697.6 8.3 fusion.237
  705.9 8.3 fusion.234
  717.2 6.2 bitcast_convert_fusion
  725.4 3.9 fusion.240
  730.3 43.7 %reduce-scatter.20.cloned.1.call-done = bf16[1,256,1280]{2,1,0:T(8,128)(2,1)} async-done(((bf16[8,256,1280]{2,1,0:T(8,128)(2,1)}), bf16[1,256,1280]{2,1,0:T(8,128)(2,1)}) %reduce-scatter.20.cloned.1.call-update) | async-done | bytes 655376 | tf_op jit(solution)/shard_map/reduce_scatter | solution.py:72
  777.9 10.9 %convolution_bitcast_fusion.3 = f32[1,1280,640]{2,1,0:T(8,128)} fusion(bf16[8,256,640]{2,1,0:T(8,128)(2,1)} %copy-done.36, f32[8,256,1280]{2,1,0:T(8,128)} %param.10, f32[8,256]{1,0:T(8,128)S(1)} %copy-done.23), kind=kOutput, calls=%fused_computation.107 | convolution fusion | flops 3360686080 | bytes 16392192 | tf_op jit(solution)/shard_map/bsh,bsf->hf/dot_general | solution.py:26
  788.8 11.4 %convolution_bitcast_fusion = f32[1,640,1280]{2,1,0:T(8,128)} fusion(f32[8,256,1280]{2,1,0:T(8,128)} %param.13, f32[8,256,640]{2,1,0:T(8,128)} %fusion.138), kind=kOutput, calls=%fused_computation.104 | convolution fusion | flops 3369861120 | bytes 19005440 | tf_op jit(solution)/shard_map/bsf,bsh->fh/dot_general | solution.py:26
  800.2 4.1 fusion.97
  804.3 9.0 fusion.73
  813.3 5.7 fusion.94
  819.1 7.3 fusion.79
  826.4 6.2 convolution_bitcast_fusion.4
  832.6 6.4 convolution_bitcast_fusion.5
  839.0 7.5 pad_maximum_fusion
  846.5 9.9 convolution_bitcast_fusion.1
  856.4 8.4 convolution_bitcast_fusion.2
  864.8 7.6 pad_maximum_fusion.1
  883.4 13.8 %bitcast_subtract_fusion = f32[8,256,1280]{2,1,0:T(8,128)} fusion(f32[1,8,256,1280]{3,2,1,0:T(8,128)} %param.14, bf16[8,8,256,2,80]{2,4,3,1,0:T(8,128)(2,1)} %bitcast.387, bf16[8,2,80,1280]{3,2,1,0:T(8,128)(2,1)} %all-gather.14.cloned.1.call-done), kind=kOutput, calls=%fused_computation.9 | convolution fusion | flops 6713507840 | bytes 29491200 | tf_op jit(solution)/shard_map/dbqne,dneh->bqh/dot_general | solution.py:26
  897.3 6.7 all-gather.24.cloned.1.call-done
  904.0 60.9 %all-gather.28.cloned.1.call-done = f32[8,256,1280]{2,1,0:T(8,128)} async-done(((f32[1,256,1280]{2,1,0:T(8,128)}), f32[8,256,1280]{2,1,0:T(8,128)}) %all-gather.28.cloned.1.call-update) | async-done | bytes 10485776 | tf_op jit(solution)/shard_map/all_gather | solution.py:76
  964.9 9.6 copy.156
  974.6 4.1 copy.157
  978.7 8.8 copy.158
  (202 shorter events, 80.0 us)
Async XLA Ops:
  7.2 86.0 %reduce-scatter.10.cloned.1.call-start = ((), (), s32[]{:S(2)}) async-start(), calls=%async_computation.10 | async-start | bytes 5898240 | tf_op jit(solution)/shard_map/reduce_scatter | solution.py:72
  7.2 7.0 copy-start.1
  7.2 14.7 %slice-start.8 = ((s8[10485760]{0:T(1024)(128)(4,1)}), s8[4194304]{0:T(1024)(128)(4,1)S(1)}, s32[]{:S(2)}) async-start(s8[10485760]{0:T(1024)(128)(4,1)} %bitcast.383), calls=%async_computation.32 | async-start | bytes 8388608
  14.2 7.7 slice-start.9
  14.2 7.7 slice-start.10
  39.8 132.6 %reduce-scatter.12.cloned.1.call-start = ((), (), s32[]{:S(2)}) async-start(), calls=%async_computation.11 | async-start | bytes 11796480 | tf_op jit(solution)/shard_map/reduce_scatter | solution.py:72
  52.1 159.7 %all-gather.18.cloned.1.call-start = ((), (), s32[]{:S(2)}) async-start(), calls=%async_computation.13 | async-start | bytes 5898240 | tf_op jit(solution)/shard_map/all_gather | solution.py:76
  98.1 153.8 %all-gather.16.cloned.1.call-start = ((), (), s32[]{:S(2)}) async-start(), calls=%async_computation.12 | async-start | bytes 5898240 | tf_op jit(solution)/shard_map/all_gather | solution.py:76
  175.3 141.5 %reduce-scatter.16.cloned.1.call-start = ((), (), s32[]{:S(2)}) async-start(), calls=%async_computation.15 | async-start | bytes 5898240 | tf_op jit(solution)/shard_map/reduce_scatter | solution.py:72
  180.1 7.1 copy-start.24
  187.2 4.0 copy-start.16
  193.7 43.7 %copy-start.5 = (bf16[8,2,256,256]{2,3,1,0:T(8,128)(2,1)}, bf16[8,2,256,256]{2,3,1,0:T(8,128)(2,1)S(1)}, u32[]{:S(2)}) copy-start(bf16[8,2,256,256]{2,3,1,0:T(8,128)(2,1)S(1)} %fusion.314) | copy-start | bytes 6291460
  247.2 112.2 %reduce-scatter.14.cloned.1.call-start = ((), (), s32[]{:S(2)}) async-start(), calls=%async_computation.14 | async-start | bytes 5898240 | tf_op jit(solution)/shard_map/reduce_scatter | solution.py:72
  257.5 3.5 copy-start.17
  271.5 12.6 %copy-start.39 = (bf16[8,256,1,2,80]{1,4,3,0,2:T(8,128)(2,1)}, bf16[8,256,1,2,80]{1,4,3,0,2:T(8,128)(2,1)S(1)}, u32[]{:S(2)}) copy-start(bf16[8,256,1,2,80]{1,4,3,0,2:T(8,128)(2,1)S(1)} %fusion.225) | copy-start | bytes 1966084
  279.2 5.0 copy-start.40
  291.0 147.7 %reduce-scatter.8.cloned.1.call-start = ((), (), s32[]{:S(2)}) async-start(), calls=%async_computation.7 | async-start | bytes 11796480 | tf_op jit(solution)/shard_map/reduce_scatter | solution.py:72
  296.2 147.9 %copy-start.26 = (f32[8,256]{1,0:T(8,128)}, f32[8,256]{1,0:T(8,128)S(1)}, u32[]{:S(2)}) copy-start(f32[8,256]{1,0:T(8,128)S(1)} %add_rsqrt_fusion.3) | copy-start | bytes 24580
  303.8 2.4 copy-start.31
  315.3 165.1 %all-gather.20.cloned.1.call-start = ((), (), s32[]{:S(2)}) async-start(), calls=%async_computation.16 | async-start | bytes 5898240 | tf_op jit(solution)/shard_map/all_gather | solution.py:76
  316.8 121.8 %copy-start.11 = (bf16[1,256,1280]{2,1,0:T(8,128)(2,1)S(1)}, bf16[1,256,1280]{2,1,0:T(8,128)(2,1)}, u32[]{:S(2)}) copy-start(bf16[1,256,1280]{2,1,0:T(8,128)(2,1)} %reduce-scatter.16.cloned.1.call-done) | copy-start | bytes 1966084
  443.3 76.5 %all-gather.22.cloned.1.call-start = ((), (), s32[]{:S(2)}) async-start(), calls=%async_computation.17 | async-start | bytes 5898240 | tf_op jit(solution)/shard_map/all_gather | solution.py:76
  444.0 145.0 %reduce-scatter.18.cloned.1.call-start = ((), (), s32[]{:S(2)}) async-start(), calls=%async_computation.18 | async-start | bytes 5898240 | tf_op jit(solution)/shard_map/reduce_scatter | solution.py:72
  519.8 11.2 %copy-start.30 = (f32[8,256,1280]{2,1,0:T(8,128)S(1)}, f32[8,256,1280]{2,1,0:T(8,128)}, u32[]{:S(2)}) copy-start(f32[8,256,1280]{2,1,0:T(8,128)} %fusion.158) | copy-start | bytes 31457284
  538.4 52.4 %copy-start.8 = (bf16[1,256,1280]{2,1,0:T(8,128)(2,1)S(1)}, bf16[1,256,1280]{2,1,0:T(8,128)(2,1)}, u32[]{:S(2)}) copy-start(bf16[1,256,1280]{2,1,0:T(8,128)(2,1)} %reduce-scatter.10.cloned.1.call-done) | copy-start | bytes 1966084
  538.4 111.7 %all-gather.12.cloned.1.call-start = ((), (), s32[]{:S(2)}) async-start(), calls=%async_computation.8 | async-start | bytes 11796480 | tf_op jit(solution)/shard_map/all_gather | solution.py:76
  539.2 150.2 %all-gather.26.cloned.1.call-start = ((), (), s32[]{:S(2)}) async-start(), calls=%async_computation.20 | async-start | bytes 5898240 | tf_op jit(solution)/shard_map/all_gather | solution.py:76
  595.1 178.9 %reduce-scatter.20.cloned.1.call-start = ((), (), s32[]{:S(2)}) async-start(), calls=%async_computation.21 | async-start | bytes 5898240 | tf_op jit(solution)/shard_map/reduce_scatter | solution.py:72
  650.1 7.0 copy-start
  657.1 4.2 copy-start.28
  714.1 3.1 copy-start.41
  714.1 3.1 copy-start.43
  717.2 6.2 copy-start.37
  723.4 160.0 %all-gather.14.cloned.1.call-start = ((), (), s32[]{:S(2)}) async-start(), calls=%async_computation.9 | async-start | bytes 3686400 | tf_op jit(solution)/shard_map/all_gather | solution.py:132
  725.3 48.7 %copy-start.2 = (f32[1,256,1280]{2,1,0:T(8,128)S(1)}, f32[1,256,1280]{2,1,0:T(8,128)}, u32[]{:S(2)}) copy-start(f32[1,256,1280]{2,1,0:T(8,128)} %get-tuple-element.18) | copy-start | bytes 3932164
  725.3 158.1 %all-gather.30.cloned.1.call-start = ((), (), s32[]{:S(2)}) async-start(), calls=%async_computation.23 | async-start | bytes 5898240 | tf_op jit(solution)/shard_map/all_gather | solution.py:131
  729.3 174.8 %all-gather.24.cloned.1.call-start = ((), (), s32[]{:S(2)}) async-start(), calls=%async_computation.19 | async-start | bytes 11796480 | tf_op jit(solution)/shard_map/all_gather | solution.py:76
  729.8 48.1 %copy-start.23 = (f32[8,256]{1,0:T(8,128)S(1)}, f32[8,256]{1,0:T(8,128)}, u32[]{:S(2)}) copy-start(f32[8,256]{1,0:T(8,128)} %copy-done.22) | copy-start | bytes 24580
  729.8 235.1 %all-gather.28.cloned.1.call-start = ((), (), s32[]{:S(2)}) async-start(), calls=%async_computation.22 | async-start | bytes 11796480 | tf_op jit(solution)/shard_map/all_gather | solution.py:76
  788.8 11.4 %copy-start.6 = (bf16[8,2,256,256]{2,3,1,0:T(8,128)(2,1)S(1)}, bf16[8,2,256,256]{2,3,1,0:T(8,128)(2,1)}, u32[]{:S(2)}) copy-start(bf16[8,2,256,256]{2,3,1,0:T(8,128)(2,1)} %copy-done.5) | copy-start | bytes 6291460
  800.2 4.1 copy-start.25
  813.3 13.0 %slice-start.3 = ((s8[10485760]{0:T(1024)(128)(4,1)}), s8[2097152]{0:T(1024)(128)(4,1)S(1)}, s32[]{:S(2)}) async-start(s8[10485760]{0:T(1024)(128)(4,1)} %bitcast.379), calls=%async_computation.27 | async-start | bytes 4194304
  819.1 7.3 slice-start.4
  819.1 7.3 slice-start.5
  819.1 7.3 copy-start.27
  819.1 7.3 copy-start.33
  826.4 6.2 copy-start.35
  832.6 6.4 copy-start.10
  839.0 17.4 %slice-start.11 = ((s8[5242880]{0:T(1024)(128)(4,1)}), s8[1048576]{0:T(1024)(128)(4,1)S(1)}, s32[]{:S(2)}) async-start(s8[5242880]{0:T(1024)(128)(4,1)} %bitcast.385), calls=%async_computation.35 | async-start | bytes 2097152
  846.5 9.9 slice-start.12
  846.5 25.9 %slice-start.6 = ((s8[5242880]{0:T(1024)(128)(4,1)}), s8[4194304]{0:T(1024)(128)(4,1)S(1)}, s32[]{:S(2)}) async-start(s8[5242880]{0:T(1024)(128)(4,1)} %bitcast.381), calls=%async_computation.30 | async-start | bytes 8388608
  856.4 8.4 copy-start.9
  856.4 16.0 %slice-start.7 = ((s8[5242880]{0:T(1024)(128)(4,1)}), s8[1048576]{0:T(1024)(128)(4,1)S(1)}, s32[]{:S(2)}) async-start(s8[5242880]{0:T(1024)(128)(4,1)} %bitcast.381), calls=%async_computation.31 | async-start | bytes 2097152
  864.8 7.6 copy-start.12
  864.8 10.4 %slice-start = ((s8[10485760]{0:T(1024)(128)(4,1)}), s8[4194304]{0:T(1024)(128)(4,1)S(1)}, s32[]{:S(2)}) async-start(s8[10485760]{0:T(1024)(128)(4,1)} %bitcast.377), calls=%async_computation.24 | async-start | bytes 8388608
  864.8 10.4 %slice-start.1 = ((s8[10485760]{0:T(1024)(128)(4,1)}), s8[2097152]{0:T(1024)(128)(4,1)S(1)}, s32[]{:S(2)}) async-start(s8[10485760]{0:T(1024)(128)(4,1)} %bitcast.377), calls=%async_computation.25 | async-start | bytes 4194304
  872.4 2.8 slice-start.2
  872.4 2.8 copy-start.29
  872.4 3.4 copy-start.38
  872.4 3.7 copy-start.42
  872.4 3.8 copy-start.44
  876.3 3.5 copy-start.14
  876.3 3.5 copy-start.15
  964.9 9.7 copy-start.4
  (11 other events, 13.4 us)
Sparse Core Ops, SparseCore 0:
  39.9 53.2 reduce-scatter.9
  97.2 75.1 reduce-scatter.11
  174.8 36.9 all-gather.17
  214.0 36.9 all-gather.15
  254.8 50.3 reduce-scatter.15
  309.0 50.4 reduce-scatter.13
  363.5 75.1 reduce-scatter.7
  443.4 36.9 all-gather.19
  482.8 36.9 all-gather.21
  538.6 50.4 reduce-scatter.17
  590.9 59.2 all-gather.11
  652.4 36.9 all-gather.25
  723.6 50.3 reduce-scatter.19
  775.7 28.6 all-gather.13
  806.1 36.9 all-gather.29
  844.8 59.1 all-gather.23
  905.7 59.1 all-gather.27
